TPU v7x, 128 devices: a whole 4x4x4 slice. The times are simulated.
128 devices in a mesh: grp: 8 (over x, core), dev: 16 (over y, z).
Axes of the slice: x: 4, y: 4, z: 4, core: 2. Of those that a mesh axis runs over, the one named last changes fastest.
Arguments:
- sep_inv: bfloat16 [4096, 4096], P('grp', 'dev'), may hold values from -0.125 to 0.125
- panels: bfloat16 [8, 96, 2048, 128], P('grp', 'dev'), may hold values from -1.1953125 to 1.1953125
- diag_inverse: bfloat16 [8, 96, 768, 128], P('grp', 'dev'), may hold values from -6 to 6
- widths: int32 [8, 32], P('grp'), may hold values from 1 to 6, 96 in all within a row
- ancestors: int32 [8, 32, 16], P('grp'), may hold values from 0 to 31, as said below
Outputs:
- off_diag: bfloat16 [8, 96, 2048, 128], P('grp', 'dev')
- diag_panels: bfloat16 [8, 96, 768, 128], P('grp', 'dev')
Inputs may be any that keep to these rules, and one draw needn't show every extreme that they name: `widths`: each row of a subtree sums to 96. `ancestors`: each supernode's list holds 16 different separator tile numbers in increasing order.
All inputs are finite; a program needn't handle non-finite values.
Results may differ from a plain program's by a relative error of at most 0.0046.
Values may be sent and summed in bfloat16 or wider, within the bound.
A program may use at most 320 MiB of HBM per device.

v0:
```python
import jax
import jax.numpy as jnp
from jax import lax
from jax.sharding import PartitionSpec as P


def extended_2(cells, sides, width):
    for axis, dim in sides:
        count = lax.axis_size(axis)
        ends = count - 1
        head = lax.slice_in_dim(cells, 0, width, axis=dim)
        tail = lax.slice_in_dim(cells, cells.shape[dim] - width, cells.shape[dim], axis=dim)
        cells = jnp.concatenate(
            [
                lax.ppermute(tail, axis, [(i, (i + 1) % count) for i in range(ends)]),
                cells,
                lax.ppermute(head, axis, [((i + 1) % count, i) for i in range(ends)]),
            ],
            axis=dim,
        )
    return cells


def on_device(sep_inv, panels, diag_inverse, widths, ancestors):
    group_count = lax.axis_size("grp")
    device_count = lax.axis_size("dev")
    rows_local = sep_inv.shape[0]
    cols_local = sep_inv.shape[1]
    stacked = lax.all_gather(sep_inv[None], ("grp", "dev"), axis=0, tiled=True)
    whole_sep = stacked.reshape(group_count, device_count, rows_local, cols_local)
    whole_sep = whole_sep.transpose(0, 2, 1, 3).reshape(
        group_count * rows_local, device_count * cols_local
    )
    block = panels.shape[3]
    anc_rows = panels.shape[2]
    anc_tiles = anc_rows // block
    local_units = panels.shape[1]
    max_tiles = diag_inverse.shape[2] // block
    sep_order = whole_sep.shape[0]
    count_blocks = sep_order // block
    row_tiles = whole_sep.reshape(count_blocks, block, sep_order)
    extended = extended_2(panels, (("dev", 1),), max_tiles - 1)
    width_row = widths[0]
    anc_table = ancestors[0]
    supernodes = width_row.shape[0]
    ends = jnp.cumsum(width_row)
    starts = ends - width_row
    position = lax.axis_index("dev") * local_units + jnp.arange(local_units, dtype=jnp.int32)
    owner = jnp.sum((ends[None, :] <= position[:, None]).astype(jnp.int32), axis=1)
    one_hot = (jnp.arange(supernodes, dtype=jnp.int32)[None, :] == owner[:, None]).astype(jnp.int32)
    column = position - jnp.sum(one_hot * starts[None, :], axis=1)
    width_unit = jnp.sum(one_hot * width_row[None, :], axis=1)
    blocks = jnp.sum(one_hot[:, :, None] * anc_table[None, :, :], axis=1)
    tile_ids = jnp.arange(count_blocks, dtype=jnp.int32)

    def per_unit(unit_idx):
        chosen = blocks[unit_idx]
        rows_pick = jnp.take(row_tiles, chosen, axis=0).reshape(anc_rows, sep_order)
        placing = (tile_ids[:, None] == chosen[None, :]).astype(jnp.bfloat16)
        panel_flat = panels[0, unit_idx].reshape(anc_tiles, block * block)
        spread = jnp.dot(placing, panel_flat, preferred_element_type=jnp.float32)
        spread = spread.astype(jnp.bfloat16).reshape(sep_order, block)
        product = jnp.dot(rows_pick, spread, preferred_element_type=jnp.float32)
        result_x = (-product).astype(jnp.bfloat16)
        start_at = unit_idx + max_tiles - 1 - column[unit_idx]
        related = lax.dynamic_slice_in_dim(extended[0], start_at, max_tiles, 0)
        inner = jnp.einsum("jrb,rc->jbc", related, result_x, preferred_element_type=jnp.float32)
        keep = (jnp.arange(max_tiles, dtype=jnp.int32) < width_unit[unit_idx]).astype(jnp.float32)
        diag_block = (
            diag_inverse[0, unit_idx].astype(jnp.float32).reshape(max_tiles, block, block) - inner
        ) * keep[:, None, None]
        return (result_x, diag_block.reshape(max_tiles * block, block).astype(jnp.bfloat16))

    off_diag, diag_panels = lax.map(per_unit, jnp.arange(local_units, dtype=jnp.int32))
    return (off_diag[None], diag_panels[None])


def solution(mesh):
    placed = (
        P("grp", "dev"),
        P("grp", "dev", None, None),
        P("grp", "dev", None, None),
        P("grp", None),
        P("grp", None, None),
    )
    return jax.shard_map(
        on_device,
        mesh=mesh,
        in_specs=placed,
        out_specs=(P("grp", "dev", None, None), P("grp", "dev", None, None)),
        check_vma=False,
    )
```

profile of v0, /device:TPU:1, one launch (start us, length us, event | category | flops | bytes accessed | tf_op | source)
XLA Modules:
  0.0 488.8 jit_solution(15844366094010139155)
XLA Ops:
  7.9 3.2 copy.21
  11.1 3.0 fusion.24
  14.1 5.9 %collective-permute-start = (bf16[1,5,2048,128]{2,3,1,0:T(8,128)(2,1)}, bf16[1,5,2048,128]{2,3,1,0:T(8,128)(2,1)}, u32[]{:S(2)}, u32[]{:S(2)}) collective-permute-start(bf16[1,5,2048,128]{2,3,1,0:T(8,128)(2,1)} %get-tuple-element.293), channel_id=1, source_target_pairs={{0,1},{1,2},{2,3},{3,4},{4,5},{5,6},{6,7},{7,8},{8,9},{9,10},{10,1... | collective-permute-start | bytes 7864328 | tf_op jit(solution)/shard_map/ppermute | solution.py:15
  22.2 54.9 %collective-permute-done = bf16[1,5,2048,128]{2,3,1,0:T(8,128)(2,1)} collective-permute-done((bf16[1,5,2048,128]{2,3,1,0:T(8,128)(2,1)}, bf16[1,5,2048,128]{2,3,1,0:T(8,128)(2,1)}, u32[]{:S(2)}, u32[]{:S(2)}) %collective-permute-start) | collective-permute-done | bytes 2621472 | tf_op jit(solution)/shard_map/ppermute | solution.py:15
  77.1 5.4 %collective-permute-done.1 = bf16[1,5,2048,128]{2,3,1,0:T(8,128)(2,1)} collective-permute-done((bf16[1,5,2048,128]{2,3,1,0:T(8,128)(2,1)}, bf16[1,5,2048,128]{2,3,1,0:T(8,128)(2,1)}, u32[]{:S(2)}, u32[]{:S(2)}) %collective-permute-start.1) | collective-permute-done | bytes 2621472 | tf_op jit(solution)/shard_map/ppermute | solution.py:17
  82.5 6.3 %pad_maximum_fusion = bf16[1,16,2048,128]{2,3,1,0:T(8,128)(2,1)} fusion(bf16[1,5,2048,128]{2,3,1,0:T(8,128)(2,1)} %collective-permute-done.1, bf16[1,6,2048,128]{2,3,1,0:T(8,128)(2,1)S(1)} %copy.21, bf16[1,5,2048,128]{2,3,1,0:T(8,128)(2,1)} %collective-permute-done), kind=kLoop, calls=%fused_computation.29 | loop fusion | flops 8388608 | bytes 16777216 | tf_op jit(solution)/shard_map/concatenate | solution.py:13
  88.8 80.5 %all-gather.3.cloned.1.call-done = bf16[65536,256]{1,0:T(8,128)(2,1)} async-done(((bf16[512,256]{1,0:T(8,128)(2,1)}), bf16[65536,256]{1,0:T(8,128)(2,1)}) %all-gather.3.cloned.1.call-update) | async-done | bytes 33554448 | tf_op jit(solution)/shard_map/all_gather | solution.py:29
  169.3 31.2 %copy.25 = bf16[8,16,512,256]{3,1,2,0:T(8,128)(2,1)} copy(bf16[8,16,512,256]{3,2,1,0:T(8,128)(2,1)} %bitcast.82) | data formatting | bytes 67108864 | tf_op jit(solution)/shard_map/reshape | solution.py:30
  200.5 49.9 %reshape_reshape.3 = bf16[32,128,4096]{2,1,0:T(8,128)(2,1)} reshape(bf16[8,512,16,256]{3,2,1,0:T(8,128)(2,1)} %bitcast.81) | data formatting | bytes 67108864 | tf_op jit(solution)/shard_map/reshape;reshape | solution.py:41
  250.4 231.6 %while.17 = (s32[]{:T(128)}, bf16[6,2048,128]{2,1,0:T(8,128)(2,1)}, bf16[6,768,128]{2,1,0:T(8,128)(2,1)}, s32[6]{0:T(128)S(1)}, s32[6,16]{1,0:T(8,128)S(1)}, /*i...) while((s32[]{:T(128)}, bf16[6,2048,128]{2,1,0:T(8,128)(2,1)}, ...), condition=%wide.region_6.7_spmd.clone, body=%wide.region_5.6_spmd.clone.sunk | while | flops 2576746240 | bytes 96605016 | solution.py:74
  259.7 11.8 %gather_fusion = bf16[16,128,4096]{2,1,0:T(8,128)(2,1)} fusion(bf16[32,128,4096]{2,1,0:T(8,128)(2,1)} %get-tuple-element.407, s32[1024]{0:T(1024)S(1)} %pad_clamp_fusion.2), kind=kCustom, calls=%fused_computation.clone.clone.1 | custom fusion | bytes 33554496 | tf_op jit(solution)/shard_map/while/body/eval_jaxpr/jit(_take)/gather | solution.py:58
  271.4 8.5 %broadcast_select_fusion.2 = bf16[16,128,4096]{2,1,0:T(8,128)(2,1)S(1)} fusion(bf16[16,128,4096]{2,1,0:T(8,128)(2,1)} %gather_fusion, pred[16]{0:T(512)(128)(4,1)S(1)} %get-tuple-element.366), kind=kLoop, calls=%fused_computation.3.clone.1 | loop fusion | flops 8388608 | bytes 33554448 | tf_op jit(solution)/shard_map/while/body/eval_jaxpr/jit(_take)/select_n | solution.py:58
  280.0 5.5 %bitcast_dynamic-update-slice_fusion.4 = (bf16[6,2048,128]{2,1,0:T(8,128)(2,1)}, bf16[2048,128]{1,0:T(8,128)(2,1)S(1)}) fusion(bf16[6,2048,128]{2,1,0:T(8,128)(2,1)} %get-tuple-element.387, s32[]{:T(128)S(6)} %copy.31, bf16[2048,4096]{1,0:T(8,128)(2,1)S(1)} %bitcast.80, bf16[4096,128]{1,0:T(8,128)(2,1)S(1)} %reshape.215), kind=kOutput, calls=%fused_computation.13.clone.1 | convolution fusion | flops 2148007936 | bytes 18874372 | tf_op jit(solution)/shard_map/while/body/eval_jaxpr/dot_general | solution.py:63
  285.4 2.9 fusion.41
  298.3 11.8 %gather_fusion = bf16[16,128,4096]{2,1,0:T(8,128)(2,1)} fusion(bf16[32,128,4096]{2,1,0:T(8,128)(2,1)} %get-tuple-element.407, s32[1024]{0:T(1024)S(1)} %pad_clamp_fusion.2), kind=kCustom, calls=%fused_computation.clone.clone.1 | custom fusion | bytes 33554496 | tf_op jit(solution)/shard_map/while/body/eval_jaxpr/jit(_take)/gather | solution.py:58
  310.0 8.5 %broadcast_select_fusion.2 = bf16[16,128,4096]{2,1,0:T(8,128)(2,1)S(1)} fusion(bf16[16,128,4096]{2,1,0:T(8,128)(2,1)} %gather_fusion, pred[16]{0:T(512)(128)(4,1)S(1)} %get-tuple-element.366), kind=kLoop, calls=%fused_computation.3.clone.1 | loop fusion | flops 8388608 | bytes 33554448 | tf_op jit(solution)/shard_map/while/body/eval_jaxpr/jit(_take)/select_n | solution.py:58
  318.5 5.5 %bitcast_dynamic-update-slice_fusion.4 = (bf16[6,2048,128]{2,1,0:T(8,128)(2,1)}, bf16[2048,128]{1,0:T(8,128)(2,1)S(1)}) fusion(bf16[6,2048,128]{2,1,0:T(8,128)(2,1)} %get-tuple-element.387, s32[]{:T(128)S(6)} %copy.31, bf16[2048,4096]{1,0:T(8,128)(2,1)S(1)} %bitcast.80, bf16[4096,128]{1,0:T(8,128)(2,1)S(1)} %reshape.215), kind=kOutput, calls=%fused_computation.13.clone.1 | convolution fusion | flops 2148007936 | bytes 18874372 | tf_op jit(solution)/shard_map/while/body/eval_jaxpr/dot_general | solution.py:63
  336.8 11.8 %gather_fusion = bf16[16,128,4096]{2,1,0:T(8,128)(2,1)} fusion(bf16[32,128,4096]{2,1,0:T(8,128)(2,1)} %get-tuple-element.407, s32[1024]{0:T(1024)S(1)} %pad_clamp_fusion.2), kind=kCustom, calls=%fused_computation.clone.clone.1 | custom fusion | bytes 33554496 | tf_op jit(solution)/shard_map/while/body/eval_jaxpr/jit(_take)/gather | solution.py:58
  348.6 8.5 %broadcast_select_fusion.2 = bf16[16,128,4096]{2,1,0:T(8,128)(2,1)S(1)} fusion(bf16[16,128,4096]{2,1,0:T(8,128)(2,1)} %gather_fusion, pred[16]{0:T(512)(128)(4,1)S(1)} %get-tuple-element.366), kind=kLoop, calls=%fused_computation.3.clone.1 | loop fusion | flops 8388608 | bytes 33554448 | tf_op jit(solution)/shard_map/while/body/eval_jaxpr/jit(_take)/select_n | solution.py:58
  357.1 5.5 %bitcast_dynamic-update-slice_fusion.4 = (bf16[6,2048,128]{2,1,0:T(8,128)(2,1)}, bf16[2048,128]{1,0:T(8,128)(2,1)S(1)}) fusion(bf16[6,2048,128]{2,1,0:T(8,128)(2,1)} %get-tuple-element.387, s32[]{:T(128)S(6)} %copy.31, bf16[2048,4096]{1,0:T(8,128)(2,1)S(1)} %bitcast.80, bf16[4096,128]{1,0:T(8,128)(2,1)S(1)} %reshape.215), kind=kOutput, calls=%fused_computation.13.clone.1 | convolution fusion | flops 2148007936 | bytes 18874372 | tf_op jit(solution)/shard_map/while/body/eval_jaxpr/dot_general | solution.py:63
  362.6 2.9 fusion.41
  375.4 11.8 %gather_fusion = bf16[16,128,4096]{2,1,0:T(8,128)(2,1)} fusion(bf16[32,128,4096]{2,1,0:T(8,128)(2,1)} %get-tuple-element.407, s32[1024]{0:T(1024)S(1)} %pad_clamp_fusion.2), kind=kCustom, calls=%fused_computation.clone.clone.1 | custom fusion | bytes 33554496 | tf_op jit(solution)/shard_map/while/body/eval_jaxpr/jit(_take)/gather | solution.py:58
  387.2 8.5 %broadcast_select_fusion.2 = bf16[16,128,4096]{2,1,0:T(8,128)(2,1)S(1)} fusion(bf16[16,128,4096]{2,1,0:T(8,128)(2,1)} %gather_fusion, pred[16]{0:T(512)(128)(4,1)S(1)} %get-tuple-element.366), kind=kLoop, calls=%fused_computation.3.clone.1 | loop fusion | flops 8388608 | bytes 33554448 | tf_op jit(solution)/shard_map/while/body/eval_jaxpr/jit(_take)/select_n | solution.py:58
  395.7 5.5 %bitcast_dynamic-update-slice_fusion.4 = (bf16[6,2048,128]{2,1,0:T(8,128)(2,1)}, bf16[2048,128]{1,0:T(8,128)(2,1)S(1)}) fusion(bf16[6,2048,128]{2,1,0:T(8,128)(2,1)} %get-tuple-element.387, s32[]{:T(128)S(6)} %copy.31, bf16[2048,4096]{1,0:T(8,128)(2,1)S(1)} %bitcast.80, bf16[4096,128]{1,0:T(8,128)(2,1)S(1)} %reshape.215), kind=kOutput, calls=%fused_computation.13.clone.1 | convolution fusion | flops 2148007936 | bytes 18874372 | tf_op jit(solution)/shard_map/while/body/eval_jaxpr/dot_general | solution.py:63
  401.2 2.9 fusion.41
  414.0 11.8 %gather_fusion = bf16[16,128,4096]{2,1,0:T(8,128)(2,1)} fusion(bf16[32,128,4096]{2,1,0:T(8,128)(2,1)} %get-tuple-element.407, s32[1024]{0:T(1024)S(1)} %pad_clamp_fusion.2), kind=kCustom, calls=%fused_computation.clone.clone.1 | custom fusion | bytes 33554496 | tf_op jit(solution)/shard_map/while/body/eval_jaxpr/jit(_take)/gather | solution.py:58
  425.8 8.5 %broadcast_select_fusion.2 = bf16[16,128,4096]{2,1,0:T(8,128)(2,1)S(1)} fusion(bf16[16,128,4096]{2,1,0:T(8,128)(2,1)} %gather_fusion, pred[16]{0:T(512)(128)(4,1)S(1)} %get-tuple-element.366), kind=kLoop, calls=%fused_computation.3.clone.1 | loop fusion | flops 8388608 | bytes 33554448 | tf_op jit(solution)/shard_map/while/body/eval_jaxpr/jit(_take)/select_n | solution.py:58
  434.3 5.5 %bitcast_dynamic-update-slice_fusion.4 = (bf16[6,2048,128]{2,1,0:T(8,128)(2,1)}, bf16[2048,128]{1,0:T(8,128)(2,1)S(1)}) fusion(bf16[6,2048,128]{2,1,0:T(8,128)(2,1)} %get-tuple-element.387, s32[]{:T(128)S(6)} %copy.31, bf16[2048,4096]{1,0:T(8,128)(2,1)S(1)} %bitcast.80, bf16[4096,128]{1,0:T(8,128)(2,1)S(1)} %reshape.215), kind=kOutput, calls=%fused_computation.13.clone.1 | convolution fusion | flops 2148007936 | bytes 18874372 | tf_op jit(solution)/shard_map/while/body/eval_jaxpr/dot_general | solution.py:63
  439.8 2.9 fusion.41
  452.7 11.8 %gather_fusion = bf16[16,128,4096]{2,1,0:T(8,128)(2,1)} fusion(bf16[32,128,4096]{2,1,0:T(8,128)(2,1)} %get-tuple-element.407, s32[1024]{0:T(1024)S(1)} %pad_clamp_fusion.2), kind=kCustom, calls=%fused_computation.clone.clone.1 | custom fusion | bytes 33554496 | tf_op jit(solution)/shard_map/while/body/eval_jaxpr/jit(_take)/gather | solution.py:58
  464.4 8.5 %broadcast_select_fusion.2 = bf16[16,128,4096]{2,1,0:T(8,128)(2,1)S(1)} fusion(bf16[16,128,4096]{2,1,0:T(8,128)(2,1)} %gather_fusion, pred[16]{0:T(512)(128)(4,1)S(1)} %get-tuple-element.366), kind=kLoop, calls=%fused_computation.3.clone.1 | loop fusion | flops 8388608 | bytes 33554448 | tf_op jit(solution)/shard_map/while/body/eval_jaxpr/jit(_take)/select_n | solution.py:58
  472.9 5.5 %bitcast_dynamic-update-slice_fusion.4 = (bf16[6,2048,128]{2,1,0:T(8,128)(2,1)}, bf16[2048,128]{1,0:T(8,128)(2,1)S(1)}) fusion(bf16[6,2048,128]{2,1,0:T(8,128)(2,1)} %get-tuple-element.387, s32[]{:T(128)S(6)} %copy.31, bf16[2048,4096]{1,0:T(8,128)(2,1)S(1)} %bitcast.80, bf16[4096,128]{1,0:T(8,128)(2,1)S(1)} %reshape.215), kind=kOutput, calls=%fused_computation.13.clone.1 | convolution fusion | flops 2148007936 | bytes 18874372 | tf_op jit(solution)/shard_map/while/body/eval_jaxpr/dot_general | solution.py:63
  (100 shorter events, 47.9 us)
Async XLA Ops:
  7.2 162.2 %all-gather.3.cloned.1.call-start = ((), (), s32[]{:S(2)}) async-start(), calls=%async_computation | async-start | bytes 33816576 | tf_op jit(solution)/shard_map/all_gather | solution.py:29
  11.1 10.2 %copy-start.1 = (s32[1,32]{1,0:T(1,128)S(1)}, s32[1,32]{1,0:T(1,128)}, u32[]{:S(2)}) copy-start(s32[1,32]{1,0:T(1,128)} %param.10) | copy-start | bytes 388
  11.1 10.7 %copy-start = (s32[1,32,16]{1,2,0:T(8,128)S(1)}, s32[1,32,16]{1,2,0:T(8,128)}, u32[]{:S(2)}) copy-start(s32[1,32,16]{1,2,0:T(8,128)} %param.11) | copy-start | bytes 6148
  14.1 63.0 %collective-permute-start = (bf16[1,5,2048,128]{2,3,1,0:T(8,128)(2,1)}, bf16[1,5,2048,128]{2,3,1,0:T(8,128)(2,1)}, u32[]{:S(2)}, u32[]{:S(2)}) collective-permute-start(bf16[1,5,2048,128]{2,3,1,0:T(8,128)(2,1)} %get-tuple-element.293), channel_id=1, source_target_pairs={{0,1},{1,2},{2,3},{3,4},{4,5},{5,6},{6,7},{7,8},{8,9},{9,10},{10,1... | collective-permute-start | bytes 7864328 | tf_op jit(solution)/shard_map/ppermute | solution.py:15
  20.0 62.5 %collective-permute-start.1 = (bf16[1,5,2048,128]{2,3,1,0:T(8,128)(2,1)}, bf16[1,5,2048,128]{2,3,1,0:T(8,128)(2,1)}, u32[]{:S(2)}, u32[]{:S(2)}) collective-permute-start(bf16[1,5,2048,128]{2,3,1,0:T(8,128)(2,1)} %get-tuple-element.294), channel_id=1, source_target_pairs={{1,0},{2,1},{3,2},{4,3},{5,4},{6,5},{7,6},{8,7},{9,8},{10,9},{11,1... | collective-permute-start | bytes 7864328 | tf_op jit(solution)/shard_map/ppermute | solution.py:17
Sparse Core Ops, SparseCore 0:
  11.1 158.1 all-gather.2
where the time goes:
time: 492 us; the launch traced here: 489 us
  local copies, waits for them, and re-layouts  191 us (39%)
  waiting for transfers between devices  141 us (29%)
  other arithmetic  62.4 us (13%)
  matrix products  52.4 us (11%)
  loops' own time  20.7 us (4%)
  between operations  14.1 us (3%)
  starting transfers between devices  7.21 us (1%)
    all_gather x1, waiting for transfers between devices, on_device(): stacked = lax.all_gather(sep_inv[None], ('grp', 'dev'), axis=0, tiled=True)  80.5 us
    gather x6, local copies, waits for them, and re-layouts, per_unit(): rows_pick = jnp.take(row_tiles, chosen, axis=0).reshape(anc_rows, sep_order)  70.6 us
    ppermute x1, waiting for transfers between devices, extended_2(): lax.ppermute(tail, axis, [(i, (i + 1) % count) for i in range(ends)])  54.9 us
    select_n x12, other arithmetic, per_unit(): rows_pick = jnp.take(row_tiles, chosen, axis=0).reshape(anc_rows, sep_order)  51.1 us
    another operation x1, local copies, waits for them, and re-layouts, on_device(): row_tiles = whole_sep.reshape(count_blocks, block, sep_order)  49.9 us
    dot_general x6, matrix products, per_unit(): product = jnp.dot(rows_pick, spread, preferred_element_type=jnp.float32)  32.8 us
    reshape x1, local copies, waits for them, and re-layouts, on_device(): stacked.reshape(group_count, device_count, rows_local, cols_local)  31.2 us
    another operation x1, loops' own time, on_device(): lax.map(per_unit, jnp.arange(local_units, dtype=jnp.int32))  20.7 us
  transfers between devices with their start and end apart: 3, of which 3 were waited for; matrix products, arithmetic and copies ran while one was open for 3% of the time, Pallas kernels for 0%

commit v1 on v0

--- a/solution.py
+++ b/solution.py
@@ -2,6 +2,13 @@
 import jax.numpy as jnp
 from jax import lax
 from jax.sharding import PartitionSpec as P
+
+
+def swapped_in(block, name, along):
+    size = lax.axis_size(name)
+    blocks = jnp.stack([block for _ in range(size)])
+    blocks = lax.all_to_all(blocks, name, split_axis=0, concat_axis=0)
+    return jnp.concatenate(blocks, axis=along)
 
 
 def extended_2(cells, sides, width):
@@ -26,7 +33,7 @@
     device_count = lax.axis_size("dev")
     rows_local = sep_inv.shape[0]
     cols_local = sep_inv.shape[1]
-    stacked = lax.all_gather(sep_inv[None], ("grp", "dev"), axis=0, tiled=True)
+    stacked = swapped_in(sep_inv[None], ("grp", "dev"), 0)
     whole_sep = stacked.reshape(group_count, device_count, rows_local, cols_local)
     whole_sep = whole_sep.transpose(0, 2, 1, 3).reshape(
         group_count * rows_local, device_count * cols_local

time: 492 us -> 927 us (1.88)
  the two profiles are of different devices: /device:TPU:1 before, /device:TPU:14 now
where the time goes in v1:
time: 927 us; the launch traced here: 924 us
  waiting for transfers between devices  514 us (55%)
  local copies, waits for them, and re-layouts  202 us (22%)
  other arithmetic  96 us (10%)
  matrix products  74 us (8%)
  loops' own time  19.2 us (2%)
  starting transfers between devices  18 us (2%)
    ppermute x1, waiting for transfers between devices, extended_2(): lax.ppermute(head, axis, [((i + 1) % count, i) for i in range(ends)])  500 us
    select_n x12, other arithmetic, per_unit(): rows_pick = jnp.take(row_tiles, chosen, axis=0).reshape(anc_rows, sep_order)  85 us
    gather x6, local copies, waits for them, and re-layouts, per_unit(): rows_pick = jnp.take(row_tiles, chosen, axis=0).reshape(anc_rows, sep_order)  70.6 us
    dot_general x6, matrix products, per_unit(): product = jnp.dot(rows_pick, spread, preferred_element_type=jnp.float32)  54.3 us
    another operation x1, local copies, waits for them, and re-layouts, on_device(): row_tiles = whole_sep.reshape(count_blocks, block, sep_order)  49.9 us
    transpose x1, local copies, waits for them, and re-layouts, on_device(): whole_sep.transpose(0, 2, 1, 3)  31.2 us
    another operation x1, loops' own time, on_device(): lax.map(per_unit, jnp.arange(local_units, dtype=jnp.int32))  19.2 us
  transfers between devices with their start and end apart: 3, of which 2 were waited for; matrix products, arithmetic and copies ran while one was open for 1% of the time, Pallas kernels for 0%

profile of v1, /device:TPU:14, one launch (start us, length us, event | category | flops | bytes accessed | tf_op | source)
XLA Modules:
  0.0 924.3 jit_solution(18005154484900116020)
XLA Ops:
  0.6 11.7 %stack.3 = bf16[128,1,512,256]{3,2,1,0:T(8,128)(2,1)} broadcast(bf16[512,256]{1,0:T(8,128)(2,1)} %param.7), dimensions={2,3} | broadcast | bytes 33816576 | tf_op jit(solution)/shard_map/stack | solution.py:9
  12.3 10.8 %all-to-all-start = ((bf16[128,1,512,256]{3,2,1,0:T(8,128)(2,1)}), bf16[128,1,512,256]{3,2,1,0:T(8,128)(2,1)}, u32[]{:S(2)}, u32[]{:S(2)}) async-start(bf16[128,1,512,256]{3,2,1,0:T(8,128)(2,1)} %stack.3), calls=%async_computation | async-start | bytes 67108864 | tf_op jit(solution)/shard_map/all_to_all | solution.py:10
  23.1 3.2 copy.31
  26.4 3.0 fusion.24
  29.4 5.3 collective-permute-start.1
  37.5 499.7 %collective-permute-done.1 = bf16[1,5,2048,128]{2,3,1,0:T(8,128)(2,1)} collective-permute-done((bf16[1,5,2048,128]{2,3,1,0:T(8,128)(2,1)}, bf16[1,5,2048,128]{2,3,1,0:T(8,128)(2,1)}, u32[]{:S(2)}, u32[]{:S(2)}) %collective-permute-start.1) | collective-permute-done | bytes 2621472 | tf_op jit(solution)/shard_map/ppermute | solution.py:24
  537.2 14.7 %collective-permute-done = bf16[1,5,2048,128]{2,3,1,0:T(8,128)(2,1)} collective-permute-done((bf16[1,5,2048,128]{2,3,1,0:T(8,128)(2,1)}, bf16[1,5,2048,128]{2,3,1,0:T(8,128)(2,1)}, u32[]{:S(2)}, u32[]{:S(2)}) %collective-permute-start) | collective-permute-done | bytes 2621472 | tf_op jit(solution)/shard_map/ppermute | solution.py:22
  551.9 6.3 pad_maximum_fusion
  558.3 31.2 %copy.30 = bf16[8,512,16,256]{3,2,1,0:T(8,128)(2,1)} copy(bf16[8,512,16,256]{3,1,2,0:T(8,128)(2,1)} %bitcast.3) | data formatting | bytes 67108864 | tf_op jit(solution)/shard_map/transpose | solution.py:38
  589.4 49.9 %reshape_reshape.7 = bf16[32,128,4096]{2,1,0:T(8,128)(2,1)} reshape(bf16[8,512,16,256]{3,2,1,0:T(8,128)(2,1)} %copy.30) | data formatting | bytes 67108864 | tf_op jit(solution)/shard_map/reshape;reshape | solution.py:48
  639.3 285.0 %while.17 = (s32[]{:T(128)}, bf16[6,2048,128]{2,1,0:T(8,128)(2,1)}, bf16[6,768,128]{2,1,0:T(8,128)(2,1)}, s32[6]{0:T(128)S(1)}, s32[6,16]{1,0:T(8,128)S(1)}, /*i...) while((s32[]{:T(128)}, bf16[6,2048,128]{2,1,0:T(8,128)(2,1)}, ...), condition=%wide.region_6.7_spmd.clone, body=%wide.region_5.6_spmd.clone.sunk | while | flops 2576746240 | bytes 96605016 | solution.py:81
  641.9 11.8 %gather_fusion = bf16[16,128,4096]{2,1,0:T(8,128)(2,1)} fusion(bf16[32,128,4096]{2,1,0:T(8,128)(2,1)} %get-tuple-element.407, s32[1024]{0:T(1024)S(1)} %pad_clamp_fusion.2), kind=kCustom, calls=%fused_computation.clone.clone.1 | custom fusion | bytes 33554496 | tf_op jit(solution)/shard_map/while/body/eval_jaxpr/jit(_take)/gather | solution.py:65
  653.7 14.2 %broadcast_select_fusion.2 = bf16[16,128,4096]{2,1,0:T(8,128)(2,1)} fusion(bf16[16,128,4096]{2,1,0:T(8,128)(2,1)} %gather_fusion, pred[16]{0:T(512)(128)(4,1)S(1)} %get-tuple-element.366), kind=kLoop, calls=%fused_computation.3.clone.1 | loop fusion | flops 8388608 | bytes 33554448 | tf_op jit(solution)/shard_map/while/body/eval_jaxpr/jit(_take)/select_n | solution.py:65
  670.1 9.1 bitcast_dynamic-update-slice_fusion.4
  689.4 11.8 %gather_fusion = bf16[16,128,4096]{2,1,0:T(8,128)(2,1)} fusion(bf16[32,128,4096]{2,1,0:T(8,128)(2,1)} %get-tuple-element.407, s32[1024]{0:T(1024)S(1)} %pad_clamp_fusion.2), kind=kCustom, calls=%fused_computation.clone.clone.1 | custom fusion | bytes 33554496 | tf_op jit(solution)/shard_map/while/body/eval_jaxpr/jit(_take)/gather | solution.py:65
  701.1 14.2 %broadcast_select_fusion.2 = bf16[16,128,4096]{2,1,0:T(8,128)(2,1)} fusion(bf16[16,128,4096]{2,1,0:T(8,128)(2,1)} %gather_fusion, pred[16]{0:T(512)(128)(4,1)S(1)} %get-tuple-element.366), kind=kLoop, calls=%fused_computation.3.clone.1 | loop fusion | flops 8388608 | bytes 33554448 | tf_op jit(solution)/shard_map/while/body/eval_jaxpr/jit(_take)/select_n | solution.py:65
  717.6 9.1 bitcast_dynamic-update-slice_fusion.4
  730.8 2.9 fusion.41
  736.9 11.8 %gather_fusion = bf16[16,128,4096]{2,1,0:T(8,128)(2,1)} fusion(bf16[32,128,4096]{2,1,0:T(8,128)(2,1)} %get-tuple-element.407, s32[1024]{0:T(1024)S(1)} %pad_clamp_fusion.2), kind=kCustom, calls=%fused_computation.clone.clone.1 | custom fusion | bytes 33554496 | tf_op jit(solution)/shard_map/while/body/eval_jaxpr/jit(_take)/gather | solution.py:65
  748.7 14.2 %broadcast_select_fusion.2 = bf16[16,128,4096]{2,1,0:T(8,128)(2,1)} fusion(bf16[16,128,4096]{2,1,0:T(8,128)(2,1)} %gather_fusion, pred[16]{0:T(512)(128)(4,1)S(1)} %get-tuple-element.366), kind=kLoop, calls=%fused_computation.3.clone.1 | loop fusion | flops 8388608 | bytes 33554448 | tf_op jit(solution)/shard_map/while/body/eval_jaxpr/jit(_take)/select_n | solution.py:65
  765.1 9.1 bitcast_dynamic-update-slice_fusion.4
  784.4 11.8 %gather_fusion = bf16[16,128,4096]{2,1,0:T(8,128)(2,1)} fusion(bf16[32,128,4096]{2,1,0:T(8,128)(2,1)} %get-tuple-element.407, s32[1024]{0:T(1024)S(1)} %pad_clamp_fusion.2), kind=kCustom, calls=%fused_computation.clone.clone.1 | custom fusion | bytes 33554496 | tf_op jit(solution)/shard_map/while/body/eval_jaxpr/jit(_take)/gather | solution.py:65
  796.1 14.2 %broadcast_select_fusion.2 = bf16[16,128,4096]{2,1,0:T(8,128)(2,1)} fusion(bf16[16,128,4096]{2,1,0:T(8,128)(2,1)} %gather_fusion, pred[16]{0:T(512)(128)(4,1)S(1)} %get-tuple-element.366), kind=kLoop, calls=%fused_computation.3.clone.1 | loop fusion | flops 8388608 | bytes 33554448 | tf_op jit(solution)/shard_map/while/body/eval_jaxpr/jit(_take)/select_n | solution.py:65
  812.6 9.1 bitcast_dynamic-update-slice_fusion.4
  825.8 2.9 fusion.41
  831.9 11.8 %gather_fusion = bf16[16,128,4096]{2,1,0:T(8,128)(2,1)} fusion(bf16[32,128,4096]{2,1,0:T(8,128)(2,1)} %get-tuple-element.407, s32[1024]{0:T(1024)S(1)} %pad_clamp_fusion.2), kind=kCustom, calls=%fused_computation.clone.clone.1 | custom fusion | bytes 33554496 | tf_op jit(solution)/shard_map/while/body/eval_jaxpr/jit(_take)/gather | solution.py:65
  843.7 14.2 %broadcast_select_fusion.2 = bf16[16,128,4096]{2,1,0:T(8,128)(2,1)} fusion(bf16[16,128,4096]{2,1,0:T(8,128)(2,1)} %gather_fusion, pred[16]{0:T(512)(128)(4,1)S(1)} %get-tuple-element.366), kind=kLoop, calls=%fused_computation.3.clone.1 | loop fusion | flops 8388608 | bytes 33554448 | tf_op jit(solution)/shard_map/while/body/eval_jaxpr/jit(_take)/select_n | solution.py:65
  860.1 9.1 bitcast_dynamic-update-slice_fusion.4
  879.4 11.8 %gather_fusion = bf16[16,128,4096]{2,1,0:T(8,128)(2,1)} fusion(bf16[32,128,4096]{2,1,0:T(8,128)(2,1)} %get-tuple-element.407, s32[1024]{0:T(1024)S(1)} %pad_clamp_fusion.2), kind=kCustom, calls=%fused_computation.clone.clone.1 | custom fusion | bytes 33554496 | tf_op jit(solution)/shard_map/while/body/eval_jaxpr/jit(_take)/gather | solution.py:65
  891.1 14.2 %broadcast_select_fusion.2 = bf16[16,128,4096]{2,1,0:T(8,128)(2,1)} fusion(bf16[16,128,4096]{2,1,0:T(8,128)(2,1)} %gather_fusion, pred[16]{0:T(512)(128)(4,1)S(1)} %get-tuple-element.366), kind=kLoop, calls=%fused_computation.3.clone.1 | loop fusion | flops 8388608 | bytes 33554448 | tf_op jit(solution)/shard_map/while/body/eval_jaxpr/jit(_take)/select_n | solution.py:65
  907.6 9.1 bitcast_dynamic-update-slice_fusion.4
  920.8 2.9 fusion.41
  (100 shorter events, 50.1 us)
Async XLA Ops:
  12.3 545.9 %all-to-all-start = ((bf16[128,1,512,256]{3,2,1,0:T(8,128)(2,1)}), bf16[128,1,512,256]{3,2,1,0:T(8,128)(2,1)}, u32[]{:S(2)}, u32[]{:S(2)}) async-start(bf16[128,1,512,256]{3,2,1,0:T(8,128)(2,1)} %stack.3), calls=%async_computation | async-start | bytes 67108864 | tf_op jit(solution)/shard_map/all_to_all | solution.py:10
  26.4 10.2 %copy-start.1 = (s32[1,32]{1,0:T(1,128)S(1)}, s32[1,32]{1,0:T(1,128)}, u32[]{:S(2)}) copy-start(s32[1,32]{1,0:T(1,128)} %param.10) | copy-start | bytes 388
  26.4 10.8 %copy-start = (s32[1,32,16]{1,2,0:T(8,128)S(1)}, s32[1,32,16]{1,2,0:T(8,128)}, u32[]{:S(2)}) copy-start(s32[1,32,16]{1,2,0:T(8,128)} %param.11) | copy-start | bytes 6148
  29.4 507.8 %collective-permute-start.1 = (bf16[1,5,2048,128]{2,3,1,0:T(8,128)(2,1)}, bf16[1,5,2048,128]{2,3,1,0:T(8,128)(2,1)}, u32[]{:S(2)}, u32[]{:S(2)}) collective-permute-start(bf16[1,5,2048,128]{2,3,1,0:T(8,128)(2,1)} %get-tuple-element.294), channel_id=1, source_target_pairs={{1,0},{2,1},{3,2},{4,3},{5,4},{6,5},{7,6},{8,7},{9,8},{10,9},{11,1... | collective-permute-start | bytes 7864328 | tf_op jit(solution)/shard_map/ppermute | solution.py:24
  34.6 517.3 %collective-permute-start = (bf16[1,5,2048,128]{2,3,1,0:T(8,128)(2,1)}, bf16[1,5,2048,128]{2,3,1,0:T(8,128)(2,1)}, u32[]{:S(2)}, u32[]{:S(2)}) collective-permute-start(bf16[1,5,2048,128]{2,3,1,0:T(8,128)(2,1)} %get-tuple-element.293), channel_id=1, source_target_pairs={{0,1},{1,2},{2,3},{3,4},{4,5},{5,6},{6,7},{7,8},{8,9},{9,10},{10,1... | collective-permute-start | bytes 7864328 | tf_op jit(solution)/shard_map/ppermute | solution.py:22
